TPU v7x, 32 devices: a whole 2x2x4 slice. The times are simulated.
32 devices in a mesh: ia: 4 (over y, x), ja: 4 (over z), col: 2 (over core).
Axes of the slice: x: 2, y: 2, z: 4, core: 2. Of those that a mesh axis runs over, the one named last changes fastest.
Arguments:
- pair_rep: bfloat16 [512, 512, 128], P('ia', 'ja'), may hold values from -6 to 6
- norm_gain: float32 [128], replicated, may hold values from 0.1 to 1.9
- weights: bfloat16 [4, 128, 128], P(None, None, 'col'), may hold values from -0.5 to 0.5
- residue_mask: int32 [512], replicated, may hold values 0 or 1
- product_grad: bfloat16 [512, 128, 512], P('ia', 'col', 'ja'), may hold values from -1 to 1
Outputs:
- pair_grad: bfloat16 [512, 512, 128], P('ia', 'ja')
- weight_grads: float32 [4, 128, 128], P(None, None, 'col')
All inputs are finite; a program needn't handle non-finite values.
Results may differ from a plain program's by a relative error of at most 0.0067.
Values may be sent and summed in bfloat16 or wider, within the bound.
A program may use at most 128 MiB of HBM per device.

v0:
```python
import jax
import jax.numpy as jnp
from jax import lax
from jax.sharding import PartitionSpec as P

CLIP_LIMIT = 64.0


def gate_terms(incoming, linear, gate_pre, pair_valid):
    sigmoid_gate = jax.nn.sigmoid(gate_pre)
    through = incoming * pair_valid
    return (through * sigmoid_gate, through * linear * sigmoid_gate * (1.0 - sigmoid_gate))


def on_device(pair_rep, norm_gain, weights, residue_mask, product_grad):
    row_count = pair_rep.shape[0]
    col_count = pair_rep.shape[1]
    row_first = lax.axis_index("ia") * row_count
    col_first = lax.axis_index("ja") * col_count
    validity = residue_mask.astype(jnp.float32)
    row_valid = lax.dynamic_slice_in_dim(validity, row_first, row_count)
    col_valid = lax.dynamic_slice_in_dim(validity, col_first, col_count)
    pair_valid = row_valid[:, None, None] * col_valid[None, None, :]
    floats = pair_rep.astype(jnp.float32)
    centred = floats - jnp.mean(floats, axis=-1, keepdims=True)
    inv_std = lax.rsqrt(jnp.mean(centred * centred, axis=-1, keepdims=True) + 1e-05)
    unit_rows = centred * inv_std
    normed = (unit_rows * norm_gain).astype(jnp.bfloat16)
    projected = jnp.einsum("ikd,wdc->wick", normed, weights, preferred_element_type=jnp.float32)
    left_side = (pair_valid * jax.nn.sigmoid(projected[1]) * projected[0]).astype(jnp.bfloat16)
    right_side = (pair_valid * jax.nn.sigmoid(projected[3]) * projected[2]).astype(jnp.bfloat16)
    row_panel = lax.all_gather(product_grad, "ja", axis=2, tiled=True)
    panel_part = row_panel
    grad_left = jnp.einsum(
        "icj,jck->ick",
        panel_part,
        lax.all_gather(right_side, "ia", axis=0, tiled=True),
        preferred_element_type=jnp.float32,
    )
    panel_part = row_panel
    grad_right = lax.psum_scatter(
        jnp.einsum("icj,ick->jck", panel_part, left_side, preferred_element_type=jnp.float32),
        "ia",
        scatter_dimension=0,
        tiled=True,
    )
    lin_a, gate_a = gate_terms(grad_left, projected[0], projected[1], pair_valid)
    lin_b, gate_b = gate_terms(grad_right, projected[2], projected[3], pair_valid)
    proj_grads = jnp.stack([lin_a, gate_a, lin_b, gate_b]).astype(jnp.bfloat16)
    grad_part = jnp.einsum("ikd,wick->wdc", normed, proj_grads, preferred_element_type=jnp.float32)
    input_part = jnp.einsum(
        "wick,wdc->ikd", proj_grads, weights, preferred_element_type=jnp.float32
    )
    normed_grad = lax.psum(input_part, "col")
    scaled = normed_grad * norm_gain
    pair_grad = inv_std * (
        scaled
        - jnp.mean(scaled, axis=-1, keepdims=True)
        - unit_rows * jnp.mean(scaled * unit_rows, axis=-1, keepdims=True)
    )
    summed = lax.psum(grad_part, ("ia", "ja"))
    squares = lax.psum(jnp.sum(summed * summed), "col")
    factor = jnp.minimum(1.0, CLIP_LIMIT * lax.rsqrt(squares + 1e-06))
    weight_grads = summed * factor
    return (pair_grad.astype(jnp.bfloat16), weight_grads)


def solution(mesh):
    placed = (P("ia", "ja", None), P(), P(None, None, "col"), P(), P("ia", "col", "ja"))
    return jax.shard_map(
        on_device,
        mesh=mesh,
        in_specs=placed,
        out_specs=(P("ia", "ja", None), P(None, None, "col")),
        check_vma=False,
    )
```

profile of v0, /device:TPU:0, one launch (start us, length us, event | category | flops | bytes accessed | tf_op | source)
XLA Modules:
  0.0 660.3 jit_solution(14896707460684824877)
XLA Ops:
  7.2 4.3 copy.18
  11.8 3.5 convert_reduce_fusion
  15.3 4.8 fusion.10
  20.2 4.7 convolution_bitcast_fusion
  24.9 5.9 copy-done.1
  30.8 2.6 multiply_convert_fusion.5
  33.9 129.6 %all-gather.5.cloned.1.call-done = bf16[128,64,512]{2,0,1:T(8,128)(2,1)} async-done(((bf16[128,64,128]{2,0,1:T(8,128)(2,1)}), bf16[128,64,512]{2,0,1:T(8,128)(2,1)}) %all-gather.5.cloned.1.call-update) | async-done | bytes 8388624 | tf_op jit(solution)/shard_map/all_gather | solution.py:32
  163.5 87.5 %all-gather.3.cloned.1.call-done = bf16[512,64,128]{2,1,0:T(8,128)(2,1)} async-done(((bf16[128,64,128]{2,1,0:T(8,128)(2,1)}), bf16[512,64,128]{2,1,0:T(8,128)(2,1)}) %all-gather.3.cloned.1.call-update) | async-done | bytes 8388624 | tf_op jit(solution)/shard_map/all_gather | solution.py:37
  251.0 25.2 %fusion.11 = f32[64,128,128]{2,1,0:T(8,128)} fusion(bf16[128,64,512]{2,0,1:T(8,128)(2,1)} %all-gather.5.cloned.1.call-done, bf16[512,64,128]{2,1,0:T(8,128)(2,1)} %all-gather.3.cloned.1.call-done), kind=kOutput, calls=%fused_computation.15 | convolution fusion | flops 1073741824 | bytes 20971520 | tf_op jit(solution)/shard_map/icj,jck->ick/dot_general | solution.py:34
  276.2 5.4 copy.20
  281.6 6.8 %fusion.28 = (bf16[1,128,64,128]{3,2,1,0:T(8,128)(2,1)S(1)}, bf16[1,128,64,128]{3,2,1,0:T(8,128)(2,1)}, bf16[128,64,128]{2,1,0:T(8,128)(2,1)S(1)}) fusion(f32[64,128,128]{1,0,2:T(8,128)} %copy.20, f32[128,128]{1,0:T(8,128)S(1)} %broadcast_multiply_fusion.1, f32[4,128,64,128]{3,2,0,1:T(8,128)} %copy-done.1), kind=kLoop, calls=%fused_computation.43 | loop fusion | flops 14680064 | bytes 18939904 | tf_op jit(solution)/shard_map/stack | solution.py:49
  288.5 14.1 %fusion.32 = f32[64,128,512]{2,1,0:T(8,128)} fusion(bf16[128,64,512]{2,0,1:T(8,128)(2,1)} %all-gather.5.cloned.1.call-done, bf16[128,64,128]{2,1,0:T(8,128)(2,1)S(1)} %get-tuple-element.8), kind=kOutput, calls=%fused_computation.47 | convolution fusion | flops 1073741824 | bytes 27262976 | tf_op jit(solution)/shard_map/icj,ick->jck/dot_general | solution.py:42
  302.6 16.6 %copy.23 = f32[64,128,512]{1,0,2:T(8,128)} copy(f32[64,128,512]{2,1,0:T(8,128)} %fusion.32) | data formatting | bytes 33554432 | tf_op jit(solution)/shard_map/icj,ick->jck/dot_general | solution.py:42
  319.2 153.8 %reduce-scatter.2.cloned.1.call-done = f32[128,64,128]{2,1,0:T(8,128)} async-done(((f32[512,64,128]{2,1,0:T(8,128)}), f32[128,64,128]{2,1,0:T(8,128)}) %reduce-scatter.2.cloned.1.call-update) | async-done | bytes 4194320 | tf_op jit(solution)/shard_map/reduce_scatter | solution.py:41
  473.1 6.0 fusion.30
  481.1 5.4 fusion.34
  486.6 6.5 convolution_bitcast_fusion.1
  493.1 99.0 %all-reduce.5.cloned.1.call-done = f32[4,128,64]{1,2,0:T(8,128)} async-done(((f32[4,128,64]{1,2,0:T(8,128)}), f32[4,128,64]{1,2,0:T(8,128)}) %all-reduce.5.cloned.1.call-update) | async-done | bytes 131088 | tf_op jit(solution)/shard_map/psum | solution.py:61
  592.1 1.5 multiply_reduce_fusion.1
  593.7 3.1 psum.23
  597.4 1.6 broadcast_multiply_fusion
  599.0 32.2 %all-reduce.3.cloned.1.call-done = f32[128,128,128]{2,1,0:T(8,128)} async-done(((f32[128,128,128]{2,1,0:T(8,128)}), f32[128,128,128]{2,1,0:T(8,128)}) %all-reduce.3.cloned.1.call-update) | async-done | bytes 8388624 | tf_op jit(solution)/shard_map/psum | solution.py:54
  631.2 11.6 %multiply_reduce_fusion = (f32[128,128]{1,0:T(8,128)S(1)}, f32[128,128]{1,0:T(8,128)S(1)}) fusion(f32[128,128,128]{2,1,0:T(8,128)} %all-reduce.3.cloned.1.call-done, f32[128]{0:T(128)S(1)} %copy-done.9, f32[128,128]{1,0:T(8,128)S(1)} %add_rsqrt_fusion, f32[128,128]{1,0:T(8,128)S(1)} %broadcast_multiply_fusion.4, bf16[128,128,128]{2,1,0:T(8,128)(2,1)} %param.5), kind=kLoop, calls=%fused_computation.17 | loop fusion | flops 14647296 | bytes 12845568 | tf_op jit(solution)/shard_map/reduce_sum | solution.py:58
  642.8 10.7 %fusion.9 = bf16[128,128,128]{2,1,0:T(8,128)(2,1)} fusion(bf16[128,128,128]{2,1,0:T(8,128)(2,1)S(1)} %copy-done.4, f32[128,128,128]{2,1,0:T(8,128)S(1)} %copy-done.5, f32[128,128]{1,0:T(8,128)S(1)} %get-tuple-element.11, f32[128,128]{1,0:T(8,128)S(1)} %get-tuple-element.12, f32[128]{0:T(128)S(1)} %copy-done.9, f32[128,128]{1,0:T(8,128)S(1)} %add_rsqrt_fusion, ...), kind=kLoop, calls=%fused_computation.12 | loop fusion | flops 18874368 | bytes 17039872 | tf_op jit(solution)/shard_map/convert_element_type | solution.py:65
  (37 shorter events, 3.0 us)
Async XLA Ops:
  7.2 13.0 %copy-start = (bf16[4,128,64]{1,2,0:T(8,128)(2,1)S(1)}, bf16[4,128,64]{1,2,0:T(8,128)(2,1)}, u32[]{:S(2)}) copy-start(bf16[4,128,64]{1,2,0:T(8,128)(2,1)} %param.7) | copy-start | bytes 196612
  7.2 4.4 copy-start.10
  7.2 156.3 %all-gather.5.cloned.1.call-start = ((), (), s32[]{:S(2)}) async-start(), calls=%async_computation.2 | async-start | bytes 10485760 | tf_op jit(solution)/shard_map/all_gather | solution.py:32
  11.5 239.5 %all-gather.3.cloned.1.call-start = ((), (), s32[]{:S(2)}) async-start(), calls=%async_computation.1 | async-start | bytes 10485760 | tf_op jit(solution)/shard_map/all_gather | solution.py:37
  11.6 3.7 copy-start.2
  11.8 8.4 %copy-start.9 = (f32[128]{0:T(128)S(1)}, f32[128]{0:T(128)}, u32[]{:S(2)}) copy-start(f32[128]{0:T(128)} %param.6) | copy-start | bytes 1540
  24.9 5.9 copy-start.1
  33.4 439.6 %reduce-scatter.2.cloned.1.call-start = ((), (), s32[]{:S(2)}) async-start(), calls=%async_computation.3 | async-start | bytes 20971520 | tf_op jit(solution)/shard_map/reduce_scatter | solution.py:41
  319.2 272.9 %all-reduce.5.cloned.1.call-start = ((), (), s32[]{:S(2)}) async-start(), calls=%async_computation.5 | async-start | bytes 262144 | tf_op jit(solution)/shard_map/psum | solution.py:61
  473.1 8.0 %copy-start.3 = (bf16[128,128,128]{2,1,0:T(8,128)(2,1)S(1)}, bf16[128,128,128]{2,1,0:T(8,128)(2,1)}, u32[]{:S(2)}) copy-start(bf16[128,128,128]{2,1,0:T(8,128)(2,1)} %param.5) | copy-start | bytes 12582916
  473.1 8.0 %copy-start.6 = (bf16[1,128,64,128]{3,2,1,0:T(8,128)(2,1)S(1)}, bf16[1,128,64,128]{3,2,1,0:T(8,128)(2,1)}, u32[]{:S(2)}) copy-start(bf16[1,128,64,128]{3,2,1,0:T(8,128)(2,1)} %get-tuple-element.5) | copy-start | bytes 6291460
  479.1 1.3 copy-start.7
  479.1 2.0 copy-start.8
  486.6 144.6 %all-reduce.3.cloned.1.call-start = ((), (), s32[]{:S(2)}) async-start(), calls=%async_computation.4 | async-start | bytes 16777216 | tf_op jit(solution)/shard_map/psum | solution.py:54
  631.2 11.6 %copy-start.4 = (bf16[128,128,128]{2,1,0:T(8,128)(2,1)S(1)}, bf16[128,128,128]{2,1,0:T(8,128)(2,1)}, u32[]{:S(2)}) copy-start(bf16[128,128,128]{2,1,0:T(8,128)(2,1)} %param.5) | copy-start | bytes 12582916
  631.2 11.6 %copy-start.5 = (f32[128,128,128]{2,1,0:T(8,128)S(1)}, f32[128,128,128]{2,1,0:T(8,128)}, u32[]{:S(2)}) copy-start(f32[128,128,128]{2,1,0:T(8,128)} %all-reduce.3.cloned.1.call-done) | copy-start | bytes 25165828
Sparse Core Ops, SparseCore 0:
  11.6 151.8 all-gather.4
  165.4 85.6 all-gather.2
  319.3 153.7 reduce-scatter.1
  486.7 105.3 all-reduce.4
  594.4 36.6 all-reduce.2
where the time goes:
time: 668 us; the launch traced here: 660 us
  waiting for transfers between devices  502 us (75%)
  matrix products  55.9 us (8%)
  other arithmetic  49.3 us (7%)
  local copies, waits for them, and re-layouts  34.2 us (5%)
  between operations  14.9 us (2%)
    reduce_scatter x1, waiting for transfers between devices, on_device(): lax.psum_scatter(jnp.einsum('icj,ick->jck', panel_part, left_side, prefer...  154 us
    all_gather x1, waiting for transfers between devices, on_device(): row_panel = lax.all_gather(product_grad, 'ja', axis=2, tiled=True)  130 us
    psum x1, waiting for transfers between devices, on_device(): summed = lax.psum(grad_part, ('ia', 'ja'))  99 us
    all_gather x1, waiting for transfers between devices, on_device(): lax.all_gather(right_side, 'ia', axis=0, tiled=True)  87.5 us
    psum x1, waiting for transfers between devices, on_device(): normed_grad = lax.psum(input_part, 'col')  32.2 us
    dot_general x1, matrix products, on_device(): jnp.einsum('icj,jck->ick', panel_part, lax.all_gather(right_side, 'ia', a...  25.2 us
    dot_general x1, local copies, waits for them, and re-layouts, on_device(): jnp.einsum('icj,ick->jck', panel_part, left_side, preferred_element_type=...  16.6 us
    dot_general x1, matrix products, on_device(): jnp.einsum('icj,ick->jck', panel_part, left_side, preferred_element_type=...  14.1 us
  transfers between devices with their start and end apart: 5, of which 5 were waited for; matrix products, arithmetic and copies ran while one was open for 4% of the time, Pallas kernels for 0%

commit v1 on v0

--- a/solution.py
+++ b/solution.py
@@ -58,7 +58,7 @@
         - jnp.mean(scaled, axis=-1, keepdims=True)
         - unit_rows * jnp.mean(scaled * unit_rows, axis=-1, keepdims=True)
     )
-    summed = lax.psum(grad_part, ("ia", "ja"))
+    summed = lax.psum(lax.psum(grad_part, axis_name="ia"), "ja")
     squares = lax.psum(jnp.sum(summed * summed), "col")
     factor = jnp.minimum(1.0, CLIP_LIMIT * lax.rsqrt(squares + 1e-06))
     weight_grads = summed * factor

time: 668 us -> 642 us (0.961)
  waiting for transfers between devices: 502 us -> 476 us
    psum x1 -> x2, waiting for transfers between devices: 99 us -> 72.6 us  [on_device(): summed = lax.psum(lax.psum(grad_part, axis_name='ia'), 'ja')]
  transfers between devices with their start and end apart: 5 -> 6, of which waited for: 5 -> 6; matrix products, arithmetic and copies ran while one was open for 4% -> 4% of each run, Pallas kernels for 0% -> 0%
where the time goes in v1:
time: 642 us; the launch traced here: 635 us
  waiting for transfers between devices  476 us (74%)
  matrix products  55.9 us (9%)
  other arithmetic  49.3 us (8%)
  local copies, waits for them, and re-layouts  34.2 us (5%)
  between operations  15.2 us (2%)
    reduce_scatter x1, waiting for transfers between devices, on_device(): lax.psum_scatter(jnp.einsum('icj,ick->jck', panel_part, left_side, prefer...  154 us
    all_gather x1, waiting for transfers between devices, on_device(): row_panel = lax.all_gather(product_grad, 'ja', axis=2, tiled=True)  130 us
    all_gather x1, waiting for transfers between devices, on_device(): lax.all_gather(right_side, 'ia', axis=0, tiled=True)  87.5 us
    psum x2, waiting for transfers between devices, on_device(): summed = lax.psum(lax.psum(grad_part, axis_name='ia'), 'ja')  72.6 us
    psum x1, waiting for transfers between devices, on_device(): normed_grad = lax.psum(input_part, 'col')  32.8 us
    dot_general x1, matrix products, on_device(): jnp.einsum('icj,jck->ick', panel_part, lax.all_gather(right_side, 'ia', a...  25.2 us
    dot_general x1, local copies, waits for them, and re-layouts, on_device(): jnp.einsum('icj,ick->jck', panel_part, left_side, preferred_element_type=...  16.6 us
    dot_general x1, matrix products, on_device(): jnp.einsum('icj,ick->jck', panel_part, left_side, preferred_element_type=...  14.1 us
  transfers between devices with their start and end apart: 6, of which 6 were waited for; matrix products, arithmetic and copies ran while one was open for 4% of the time, Pallas kernels for 0%

profile of v1, /device:TPU:0, one launch (start us, length us, event | category | flops | bytes accessed | tf_op | source)
XLA Modules:
  0.0 634.9 jit_solution(7055038705030784188)
XLA Ops:
  7.2 4.3 copy.18
  11.8 3.5 convert_reduce_fusion
  15.3 4.8 fusion.10
  20.2 4.7 convolution_bitcast_fusion
  24.9 5.9 copy-done.1
  30.8 2.6 multiply_convert_fusion.5
  33.9 129.6 %all-gather.5.cloned.1.call-done = bf16[128,64,512]{2,0,1:T(8,128)(2,1)} async-done(((bf16[128,64,128]{2,0,1:T(8,128)(2,1)}), bf16[128,64,512]{2,0,1:T(8,128)(2,1)}) %all-gather.5.cloned.1.call-update) | async-done | bytes 8388624 | tf_op jit(solution)/shard_map/all_gather | solution.py:32
  163.5 87.5 %all-gather.3.cloned.1.call-done = bf16[512,64,128]{2,1,0:T(8,128)(2,1)} async-done(((bf16[128,64,128]{2,1,0:T(8,128)(2,1)}), bf16[512,64,128]{2,1,0:T(8,128)(2,1)}) %all-gather.3.cloned.1.call-update) | async-done | bytes 8388624 | tf_op jit(solution)/shard_map/all_gather | solution.py:37
  251.0 25.2 %fusion.11 = f32[64,128,128]{2,1,0:T(8,128)} fusion(bf16[128,64,512]{2,0,1:T(8,128)(2,1)} %all-gather.5.cloned.1.call-done, bf16[512,64,128]{2,1,0:T(8,128)(2,1)} %all-gather.3.cloned.1.call-done), kind=kOutput, calls=%fused_computation.15 | convolution fusion | flops 1073741824 | bytes 20971520 | tf_op jit(solution)/shard_map/icj,jck->ick/dot_general | solution.py:34
  276.2 5.4 copy.20
  281.6 6.8 %fusion.28 = (bf16[1,128,64,128]{3,2,1,0:T(8,128)(2,1)S(1)}, bf16[1,128,64,128]{3,2,1,0:T(8,128)(2,1)}, bf16[128,64,128]{2,1,0:T(8,128)(2,1)S(1)}) fusion(f32[64,128,128]{1,0,2:T(8,128)} %copy.20, f32[128,128]{1,0:T(8,128)S(1)} %broadcast_multiply_fusion.1, f32[4,128,64,128]{3,2,0,1:T(8,128)} %copy-done.1), kind=kLoop, calls=%fused_computation.43 | loop fusion | flops 14680064 | bytes 18939904 | tf_op jit(solution)/shard_map/stack | solution.py:49
  288.5 14.1 %fusion.32 = f32[64,128,512]{2,1,0:T(8,128)} fusion(bf16[128,64,512]{2,0,1:T(8,128)(2,1)} %all-gather.5.cloned.1.call-done, bf16[128,64,128]{2,1,0:T(8,128)(2,1)S(1)} %get-tuple-element.8), kind=kOutput, calls=%fused_computation.47 | convolution fusion | flops 1073741824 | bytes 27262976 | tf_op jit(solution)/shard_map/icj,ick->jck/dot_general | solution.py:42
  302.6 16.6 %copy.23 = f32[64,128,512]{1,0,2:T(8,128)} copy(f32[64,128,512]{2,1,0:T(8,128)} %fusion.32) | data formatting | bytes 33554432 | tf_op jit(solution)/shard_map/icj,ick->jck/dot_general | solution.py:42
  319.2 153.8 %reduce-scatter.2.cloned.1.call-done = f32[128,64,128]{2,1,0:T(8,128)} async-done(((f32[512,64,128]{2,1,0:T(8,128)}), f32[128,64,128]{2,1,0:T(8,128)}) %reduce-scatter.2.cloned.1.call-update) | async-done | bytes 4194320 | tf_op jit(solution)/shard_map/reduce_scatter | solution.py:41
  473.1 6.0 fusion.30
  481.1 5.4 fusion.34
  486.6 42.3 %all-reduce.6.cloned.1.call-done = f32[4,128,64]{1,2,0:T(8,128)} async-done(((f32[4,128,64]{1,2,0:T(8,128)}), f32[4,128,64]{1,2,0:T(8,128)}) %all-reduce.6.cloned.1.call-update) | async-done | bytes 131088 | tf_op jit(solution)/shard_map/psum | solution.py:61
  529.0 6.5 %convolution_bitcast_fusion.1 = f32[128,128,128]{2,1,0:T(8,128)} fusion(bf16[1,128,64,128]{3,2,1,0:T(8,128)(2,1)} %copy-done.8, bf16[1,128,64,128]{3,2,1,0:T(8,128)(2,1)} %copy-done.7, bf16[1,128,64,128]{3,2,1,0:T(8,128)(2,1)} %get-tuple-element.5, bf16[1,128,64,128]{3,2,1,0:T(8,128)(2,1)S(1)} %get-tuple-element.4, bf16[4,128,64]{1,2,0:T(8,128)(2,1)S(1)} %copy-done), kind=kOutput, calls=%fused_computation.42 | convolution fusion | flops 1086324736 | bytes 16842752 | tf_op jit(solution)/shard_map/wick,wdc->ikd/dot_general | solution.py:51
  535.5 30.3 %all-reduce.8.cloned.1.call-done = f32[4,128,64]{1,2,0:T(8,128)} async-done(((f32[4,128,64]{1,2,0:T(8,128)}), f32[4,128,64]{1,2,0:T(8,128)}) %all-reduce.8.cloned.1.call-update) | async-done | bytes 131088 | tf_op jit(solution)/shard_map/psum | solution.py:61
  567.3 3.1 psum.31
  571.1 1.6 broadcast_multiply_fusion
  572.7 32.8 %all-reduce.4.cloned.1.call-done = f32[128,128,128]{2,1,0:T(8,128)} async-done(((f32[128,128,128]{2,1,0:T(8,128)}), f32[128,128,128]{2,1,0:T(8,128)}) %all-reduce.4.cloned.1.call-update) | async-done | bytes 8388624 | tf_op jit(solution)/shard_map/psum | solution.py:54
  605.5 11.6 %multiply_reduce_fusion = (f32[128,128]{1,0:T(8,128)S(1)}, f32[128,128]{1,0:T(8,128)S(1)}) fusion(f32[128,128,128]{2,1,0:T(8,128)} %all-reduce.4.cloned.1.call-done, f32[128]{0:T(128)S(1)} %copy-done.9, f32[128,128]{1,0:T(8,128)S(1)} %add_rsqrt_fusion, f32[128,128]{1,0:T(8,128)S(1)} %broadcast_multiply_fusion.4, bf16[128,128,128]{2,1,0:T(8,128)(2,1)} %param.5), kind=kLoop, calls=%fused_computation.17 | loop fusion | flops 14647296 | bytes 12845568 | tf_op jit(solution)/shard_map/reduce_sum | solution.py:58
  617.1 10.7 %fusion.9 = bf16[128,128,128]{2,1,0:T(8,128)(2,1)} fusion(bf16[128,128,128]{2,1,0:T(8,128)(2,1)S(1)} %copy-done.4, f32[128,128,128]{2,1,0:T(8,128)S(1)} %copy-done.5, f32[128,128]{1,0:T(8,128)S(1)} %get-tuple-element.11, f32[128,128]{1,0:T(8,128)S(1)} %get-tuple-element.12, f32[128]{0:T(128)S(1)} %copy-done.9, f32[128,128]{1,0:T(8,128)S(1)} %add_rsqrt_fusion, ...), kind=kLoop, calls=%fused_computation.12 | loop fusion | flops 18874368 | bytes 17039872 | tf_op jit(solution)/shard_map/convert_element_type | solution.py:65
  (40 shorter events, 4.6 us)
Async XLA Ops:
  7.2 13.0 %copy-start = (bf16[4,128,64]{1,2,0:T(8,128)(2,1)S(1)}, bf16[4,128,64]{1,2,0:T(8,128)(2,1)}, u32[]{:S(2)}) copy-start(bf16[4,128,64]{1,2,0:T(8,128)(2,1)} %param.7) | copy-start | bytes 196612
  7.2 4.4 copy-start.10
  7.2 156.3 %all-gather.5.cloned.1.call-start = ((), (), s32[]{:S(2)}) async-start(), calls=%async_computation.2 | async-start | bytes 10485760 | tf_op jit(solution)/shard_map/all_gather | solution.py:32
  11.5 239.5 %all-gather.3.cloned.1.call-start = ((), (), s32[]{:S(2)}) async-start(), calls=%async_computation.1 | async-start | bytes 10485760 | tf_op jit(solution)/shard_map/all_gather | solution.py:37
  11.6 3.7 copy-start.2
  11.8 8.4 %copy-start.9 = (f32[128]{0:T(128)S(1)}, f32[128]{0:T(128)}, u32[]{:S(2)}) copy-start(f32[128]{0:T(128)} %param.6) | copy-start | bytes 1540
  24.9 5.9 copy-start.1
  33.4 439.6 %reduce-scatter.2.cloned.1.call-start = ((), (), s32[]{:S(2)}) async-start(), calls=%async_computation.3 | async-start | bytes 20971520 | tf_op jit(solution)/shard_map/reduce_scatter | solution.py:41
  319.2 209.7 %all-reduce.6.cloned.1.call-start = ((), (), s32[]{:S(2)}) async-start(), calls=%async_computation.5 | async-start | bytes 262144 | tf_op jit(solution)/shard_map/psum | solution.py:61
  473.1 8.0 %copy-start.3 = (bf16[128,128,128]{2,1,0:T(8,128)(2,1)S(1)}, bf16[128,128,128]{2,1,0:T(8,128)(2,1)}, u32[]{:S(2)}) copy-start(bf16[128,128,128]{2,1,0:T(8,128)(2,1)} %param.5) | copy-start | bytes 12582916
  473.1 8.0 %copy-start.6 = (bf16[1,128,64,128]{3,2,1,0:T(8,128)(2,1)S(1)}, bf16[1,128,64,128]{3,2,1,0:T(8,128)(2,1)}, u32[]{:S(2)}) copy-start(bf16[1,128,64,128]{3,2,1,0:T(8,128)(2,1)} %get-tuple-element.5) | copy-start | bytes 6291460
  479.1 1.3 copy-start.7
  479.1 2.0 copy-start.8
  486.6 79.2 %all-reduce.8.cloned.1.call-start = ((), (), s32[]{:S(2)}) async-start(), calls=%async_computation.6 | async-start | bytes 262144 | tf_op jit(solution)/shard_map/psum | solution.py:61
  529.0 76.5 %all-reduce.4.cloned.1.call-start = ((), (), s32[]{:S(2)}) async-start(), calls=%async_computation.4 | async-start | bytes 16777216 | tf_op jit(solution)/shard_map/psum | solution.py:54
  605.5 11.6 %copy-start.4 = (bf16[128,128,128]{2,1,0:T(8,128)(2,1)S(1)}, bf16[128,128,128]{2,1,0:T(8,128)(2,1)}, u32[]{:S(2)}) copy-start(bf16[128,128,128]{2,1,0:T(8,128)(2,1)} %param.5) | copy-start | bytes 12582916
  605.5 11.6 %copy-start.5 = (f32[128,128,128]{2,1,0:T(8,128)S(1)}, f32[128,128,128]{2,1,0:T(8,128)}, u32[]{:S(2)}) copy-start(f32[128,128,128]{2,1,0:T(8,128)} %all-reduce.4.cloned.1.call-done) | copy-start | bytes 25165828
Sparse Core Ops, SparseCore 0:
  11.6 151.8 all-gather.4
  165.4 85.6 all-gather.2
  319.3 153.7 reduce-scatter.1
  486.7 42.2 all-reduce.5
  531.1 34.6 all-reduce.7
  568.1 37.3 all-reduce.3
